TPU v7x, 8 devices: a whole 2x2x1 slice. The times are simulated.
8 devices in a mesh: data: 8 (over z, y, x, core).
Axes of the slice: x: 2, y: 2, z: 1, core: 2. Of those that a mesh axis runs over, the one named last changes fastest.
Arguments:
- acts_in: bfloat16 [16, 3, 512, 1536], P('data')
- grad_out: bfloat16 [16, 3, 512, 1536], P('data')
- w_up: bfloat16 [3, 1536, 6144], replicated
- w_down: bfloat16 [3, 6144, 1536], replicated
- clip_norm: float32 [1], replicated
Outputs:
- output 1: bfloat16 [3, 1536, 6144], replicated
- output 2: bfloat16 [3, 6144, 1536], replicated
- output 3: bfloat16 [16, 3, 512, 1536], P('data')
All inputs are finite; a program needn't handle non-finite values.
Results may differ from a plain program's by a relative error of at most 0.0145307.
Values are sent between devices in bfloat16 or wider.
A program may use at most 1 GiB of HBM per device.

v0:
```python
import jax
import jax.numpy as jnp
from jax import lax
from jax.sharding import PartitionSpec as P, NamedSharding


def gelu_tanh(values):
    return jax.nn.gelu(values, approximate=True)


def micro_grads(x_rows, dy_rows, w_up, w_down):
    layer_count = w_up.shape[0]
    token_dims = (((0,), (0,)), ((), ()))
    right_dims = (((1,), (1,)), ((), ()))
    saved_acts = []
    hidden = x_rows
    for layer_idx in range(layer_count):
        pre_act = jnp.dot(hidden, w_up[layer_idx], preferred_element_type=jnp.float32).astype(jnp.bfloat16)
        gelu_out = gelu_tanh(pre_act.astype(jnp.float32)).astype(jnp.bfloat16)
        saved_acts.append((hidden, pre_act, gelu_out))
        hidden = (hidden.astype(jnp.float32) + jnp.dot(gelu_out, w_down[layer_idx], preferred_element_type=jnp.float32)).astype(jnp.bfloat16)
    back_grad = dy_rows
    up_grads = [None] * layer_count
    down_grads = [None] * layer_count
    for layer_idx in range(layer_count - 1, -1, -1):
        hidden, pre_act, gelu_out = saved_acts[layer_idx]
        down_grads[layer_idx] = lax.dot_general(gelu_out, back_grad, token_dims, preferred_element_type=jnp.float32)
        act_grad = lax.dot_general(back_grad, w_down[layer_idx], right_dims, preferred_element_type=jnp.float32)
        gelu_back = jax.vjp(gelu_tanh, pre_act.astype(jnp.float32))[1]
        pre_grad = gelu_back(act_grad)[0].astype(jnp.bfloat16)
        up_grads[layer_idx] = lax.dot_general(hidden, pre_grad, token_dims, preferred_element_type=jnp.float32)
        back_grad = (back_grad.astype(jnp.float32) + lax.dot_general(pre_grad, w_up[layer_idx], right_dims, preferred_element_type=jnp.float32)).astype(jnp.bfloat16)
    return up_grads, down_grads, back_grad


def solution(mesh):
    def device_step(acts_in, grad_out, w_up, w_down, clip_norm):
        micro_count, seq_count, seq_len, model_width = acts_in.shape
        tok_rows = seq_count * seq_len
        up_parts = []
        down_parts = []
        dx_blocks = []
        for micro_idx in range(micro_count):
            up_step, down_step, dx_rows = micro_grads(acts_in[micro_idx].reshape(tok_rows, model_width), grad_out[micro_idx].reshape(tok_rows, model_width), w_up, w_down)
            up_red = [lax.psum_scatter(layer_grad.astype(jnp.bfloat16), 'data', scatter_dimension=1, tiled=True).astype(jnp.float32) for layer_grad in up_step]
            down_red = [lax.psum_scatter(layer_grad.astype(jnp.bfloat16), 'data', scatter_dimension=0, tiled=True).astype(jnp.float32) for layer_grad in down_step]
            if micro_idx == 0:
                up_parts = up_red
                down_parts = down_red
            else:
                up_parts = [old_sum + new_part for old_sum, new_part in zip(up_parts, up_red)]
                down_parts = [old_sum + new_part for old_sum, new_part in zip(down_parts, down_red)]
            dx_blocks.append(dx_rows.reshape(seq_count, seq_len, model_width))
        sq_local = sum(jnp.sum(part_sum * part_sum) for part_sum in up_parts + down_parts)
        sq_total = lax.psum(sq_local, 'data')
        clip_scale = jnp.minimum(1.0, clip_norm[0] * lax.rsqrt(sq_total))
        grad_up = jnp.stack([lax.all_gather((part_sum * clip_scale).astype(jnp.bfloat16), 'data', axis=1, tiled=True) for part_sum in up_parts])
        grad_down = jnp.stack([lax.all_gather((part_sum * clip_scale).astype(jnp.bfloat16), 'data', axis=0, tiled=True) for part_sum in down_parts])
        return grad_up, grad_down, jnp.stack(dx_blocks)

    return jax.shard_map(device_step, mesh=mesh, in_specs=(P('data'), P('data'), P(), P(), P()), out_specs=(P(), P(), P('data')), check_vma=False)
```

profile of v0, /device:TPU:0, one launch (start us, length us, event | category | flops | bytes accessed | tf_op | source)
XLA Modules:
  0.0 2814.9 jit_solution(238822281064773148)
XLA Ops:
  98.7 47.1 %convolution_convert_fusion.16 = bf16[1536,6144]{1,0:T(8,128)(2,1)} fusion(bf16[1536,1536]{1,0:T(8,128)(2,1)} %add_convert_fusion.9, bf16[3,1536,6144]{2,1,0:T(8,128)(2,1)} %param.7), kind=kOutput, calls=%fused_computation.108 | convolution fusion | flops 29000466432 | bytes 42467328 | tf_op jit(solution)/shard_map/dot_general | solution.py:18
  224.3 59.5 %fusion.17 = bf16[1536,6144]{1,0:T(8,128)(2,1)} fusion(bf16[1536,6144]{1,0:T(8,128)(2,1)} %convolution_convert_fusion.15, bf16[1536,1536]{1,0:T(8,128)(2,1)} %bitcast.145, bf16[3,6144,1536]{2,1,0:T(8,128)(2,1)} %param.8), kind=kOutput, calls=%fused_computation.49 | convolution fusion | flops 29189210112 | bytes 61341696 | tf_op jit(solution)/shard_map/dot_general | solution.py:28
  324.5 59.1 %fusion.20 = bf16[1536,6144]{1,0:T(8,128)(2,1)} fusion(bf16[1536,6144]{1,0:T(8,128)(2,1)} %convolution_convert_fusion.16, bf16[1536,1536]{1,0:T(8,128)(2,1)} %add_convert_fusion.7, bf16[3,6144,1536]{2,1,0:T(8,128)(2,1)} %param.8), kind=kOutput, calls=%fused_computation.52 | convolution fusion | flops 29189210112 | bytes 61341696 | tf_op jit(solution)/shard_map/dot_general | solution.py:28
  613.9 59.6 %fusion.8 = bf16[1536,6144]{1,0:T(8,128)(2,1)} fusion(bf16[1536,6144]{1,0:T(8,128)(2,1)} %convolution_convert_fusion.12, bf16[1536,1536]{1,0:T(8,128)(2,1)} %bitcast.142, bf16[3,6144,1536]{2,1,0:T(8,128)(2,1)} %param.8), kind=kOutput, calls=%fused_computation.40 | convolution fusion | flops 29189210112 | bytes 61341696 | tf_op jit(solution)/shard_map/dot_general | solution.py:28
  714.2 59.0 %fusion.11 = bf16[1536,6144]{1,0:T(8,128)(2,1)} fusion(bf16[1536,6144]{1,0:T(8,128)(2,1)} %convolution_convert_fusion.13, bf16[1536,1536]{1,0:T(8,128)(2,1)} %add_convert_fusion.3, bf16[3,6144,1536]{2,1,0:T(8,128)(2,1)} %param.8), kind=kOutput, calls=%fused_computation.43 | convolution fusion | flops 29189210112 | bytes 61341696 | tf_op jit(solution)/shard_map/dot_general | solution.py:28
  850.4 59.3 %fusion.23 = bf16[1536,6144]{1,0:T(8,128)(2,1)} fusion(bf16[1536,6144]{1,0:T(8,128)(2,1)} %convolution_convert_fusion.17, bf16[1536,1536]{1,0:T(8,128)(2,1)} %add_convert_fusion.6, bf16[3,6144,1536]{2,1,0:T(8,128)(2,1)} %param.8), kind=kOutput, calls=%fused_computation.55 | convolution fusion | flops 29189210112 | bytes 61341696 | tf_op jit(solution)/shard_map/dot_general | solution.py:28
  986.7 59.4 %fusion.14 = bf16[1536,6144]{1,0:T(8,128)(2,1)} fusion(bf16[1536,6144]{1,0:T(8,128)(2,1)} %convolution_convert_fusion.14, bf16[1536,1536]{1,0:T(8,128)(2,1)} %add_convert_fusion.2, bf16[3,6144,1536]{2,1,0:T(8,128)(2,1)} %param.8), kind=kOutput, calls=%fused_computation.46 | convolution fusion | flops 29189210112 | bytes 61341696 | tf_op jit(solution)/shard_map/dot_general | solution.py:28
  1155.7 45.6 %convolution_convert_fusion.5 = bf16[6144,1536]{1,0:T(8,128)(2,1)} fusion(bf16[1536,1536]{1,0:T(8,128)(2,1)} %add_convert_fusion.6, bf16[1536,6144]{1,0:T(8,128)(2,1)} %convolution_convert_fusion.17), kind=kOutput, calls=%fused_computation.97 | convolution fusion | flops 29094838272 | bytes 42467328 | tf_op jit(solution)/shard_map/dot_general | solution.py:27
  1201.3 45.1 %convolution_convert_fusion.4 = bf16[6144,1536]{1,0:T(8,128)(2,1)} fusion(bf16[1536,1536]{1,0:T(8,128)(2,1)} %add_convert_fusion.2, bf16[1536,6144]{1,0:T(8,128)(2,1)} %convolution_convert_fusion.14), kind=kOutput, calls=%fused_computation.96 | convolution fusion | flops 29094838272 | bytes 42467328 | tf_op jit(solution)/shard_map/dot_general | solution.py:27
  1246.6 45.2 %convolution_convert_fusion.3 = bf16[6144,1536]{1,0:T(8,128)(2,1)} fusion(bf16[1536,1536]{1,0:T(8,128)(2,1)} %add_convert_fusion.7, bf16[1536,6144]{1,0:T(8,128)(2,1)} %convolution_convert_fusion.16), kind=kOutput, calls=%fused_computation.95 | convolution fusion | flops 29094838272 | bytes 42467328 | tf_op jit(solution)/shard_map/dot_general | solution.py:27
  1291.8 45.4 %convolution_convert_fusion.2 = bf16[6144,1536]{1,0:T(8,128)(2,1)} fusion(bf16[1536,1536]{1,0:T(8,128)(2,1)} %add_convert_fusion.3, bf16[1536,6144]{1,0:T(8,128)(2,1)} %convolution_convert_fusion.13), kind=kOutput, calls=%fused_computation.94 | convolution fusion | flops 29094838272 | bytes 42467328 | tf_op jit(solution)/shard_map/dot_general | solution.py:27
  1337.3 45.5 %convolution_convert_fusion.1 = bf16[6144,1536]{1,0:T(8,128)(2,1)} fusion(bf16[1536,1536]{1,0:T(8,128)(2,1)} %bitcast.147, bf16[1536,6144]{1,0:T(8,128)(2,1)} %convolution_convert_fusion.15), kind=kOutput, calls=%fused_computation.93 | convolution fusion | flops 29094838272 | bytes 42467328 | tf_op jit(solution)/shard_map/dot_general | solution.py:27
  1382.8 45.3 %convolution_convert_fusion = bf16[6144,1536]{1,0:T(8,128)(2,1)} fusion(bf16[1536,1536]{1,0:T(8,128)(2,1)} %bitcast.144, bf16[1536,6144]{1,0:T(8,128)(2,1)} %convolution_convert_fusion.12), kind=kOutput, calls=%fused_computation.92 | convolution fusion | flops 29094838272 | bytes 42467328 | tf_op jit(solution)/shard_map/dot_general | solution.py:27
  1448.5 115.7 %reduce-scatter.25.cloned.1.call-done = bf16[768,1536]{1,0:T(8,128)(2,1)} async-done(((bf16[6144,1536]{1,0:T(8,128)(2,1)}), bf16[768,1536]{1,0:T(8,128)(2,1)}) %reduce-scatter.25.cloned.1.call-update) | async-done | bytes 2359312 | tf_op jit(solution)/shard_map/reduce_scatter | solution.py:46
  1564.2 120.6 %reduce-scatter.27.cloned.1.call-done = bf16[768,1536]{1,0:T(8,128)(2,1)} async-done(((bf16[6144,1536]{1,0:T(8,128)(2,1)}), bf16[768,1536]{1,0:T(8,128)(2,1)}) %reduce-scatter.27.cloned.1.call-update) | async-done | bytes 2359312 | tf_op jit(solution)/shard_map/reduce_scatter | solution.py:46
  1689.8 115.7 %reduce-scatter.29.cloned.1.call-done = bf16[768,1536]{1,0:T(8,128)(2,1)} async-done(((bf16[6144,1536]{1,0:T(8,128)(2,1)}), bf16[768,1536]{1,0:T(8,128)(2,1)}) %reduce-scatter.29.cloned.1.call-update) | async-done | bytes 2359312 | tf_op jit(solution)/shard_map/reduce_scatter | solution.py:46
  1805.5 121.0 %reduce-scatter.31.cloned.1.call-done = bf16[768,1536]{1,0:T(8,128)(2,1)} async-done(((bf16[6144,1536]{1,0:T(8,128)(2,1)}), bf16[768,1536]{1,0:T(8,128)(2,1)}) %reduce-scatter.31.cloned.1.call-update) | async-done | bytes 2359312 | tf_op jit(solution)/shard_map/reduce_scatter | solution.py:46
  1931.4 115.8 %reduce-scatter.33.cloned.1.call-done = bf16[768,1536]{1,0:T(8,128)(2,1)} async-done(((bf16[6144,1536]{1,0:T(8,128)(2,1)}), bf16[768,1536]{1,0:T(8,128)(2,1)}) %reduce-scatter.33.cloned.1.call-update) | async-done | bytes 2359312 | tf_op jit(solution)/shard_map/reduce_scatter | solution.py:46
  2047.2 121.1 %reduce-scatter.35.cloned.1.call-done = bf16[768,1536]{1,0:T(8,128)(2,1)} async-done(((bf16[6144,1536]{1,0:T(8,128)(2,1)}), bf16[768,1536]{1,0:T(8,128)(2,1)}) %reduce-scatter.35.cloned.1.call-update) | async-done | bytes 2359312 | tf_op jit(solution)/shard_map/reduce_scatter | solution.py:46
  2312.7 78.2 %all-gather.11.cloned.1.call-done = bf16[1536,6144]{0,1:T(8,128)(2,1)} async-done(((bf16[1536,768]{0,1:T(8,128)(2,1)}), bf16[1536,6144]{0,1:T(8,128)(2,1)}) %all-gather.11.cloned.1.call-update) | async-done | bytes 18874384 | tf_op jit(solution)/shard_map/all_gather | solution.py:57
  2390.9 94.7 %all-gather.9.cloned.1.call-done = bf16[1536,6144]{0,1:T(8,128)(2,1)} async-done(((bf16[1536,768]{0,1:T(8,128)(2,1)}), bf16[1536,6144]{0,1:T(8,128)(2,1)}) %all-gather.9.cloned.1.call-update) | async-done | bytes 18874384 | tf_op jit(solution)/shard_map/all_gather | solution.py:57
  2523.7 72.6 %copy.12 = bf16[3,1536,6144]{2,1,0:T(8,128)(2,1)} copy(bf16[3,1536,6144]{1,2,0:T(8,128)(2,1)} %pad_maximum_fusion) | data formatting | bytes 113246208
  2596.2 78.7 %all-gather.17.cloned.1.call-done = bf16[6144,1536]{1,0:T(8,128)(2,1)} async-done(((bf16[768,1536]{1,0:T(8,128)(2,1)}), bf16[6144,1536]{1,0:T(8,128)(2,1)}) %all-gather.17.cloned.1.call-update) | async-done | bytes 18874384 | tf_op jit(solution)/shard_map/all_gather | solution.py:58
  2674.9 94.7 %all-gather.15.cloned.1.call-done = bf16[6144,1536]{1,0:T(8,128)(2,1)} async-done(((bf16[768,1536]{1,0:T(8,128)(2,1)}), bf16[6144,1536]{1,0:T(8,128)(2,1)}) %all-gather.15.cloned.1.call-update) | async-done | bytes 18874384 | tf_op jit(solution)/shard_map/all_gather | solution.py:58
  (94 shorter events, 991.0 us)
Async XLA Ops:
  7.2 1421.2 %reduce-scatter.17.cloned.1.call-start = ((), (), s32[]{:S(2)}) async-start(), calls=%async_computation.14 | async-start | bytes 21233664 | tf_op jit(solution)/shard_map/reduce_scatter | solution.py:45
  7.2 8.8 copy-start.2
  420.1 1008.3 %reduce-scatter.19.cloned.1.call-start = ((), (), s32[]{:S(2)}) async-start(), calls=%async_computation.15 | async-start | bytes 21233664 | tf_op jit(solution)/shard_map/reduce_scatter | solution.py:45
  809.9 622.9 %reduce-scatter.13.cloned.1.call-start = ((), (), s32[]{:S(2)}) async-start(), calls=%async_computation.12 | async-start | bytes 21233664 | tf_op jit(solution)/shard_map/reduce_scatter | solution.py:45
  946.2 486.6 %reduce-scatter.15.cloned.1.call-start = ((), (), s32[]{:S(2)}) async-start(), calls=%async_computation.13 | async-start | bytes 21233664 | tf_op jit(solution)/shard_map/reduce_scatter | solution.py:45
  1082.5 355.8 %reduce-scatter.21.cloned.1.call-start = ((), (), s32[]{:S(2)}) async-start(), calls=%async_computation.16 | async-start | bytes 21233664 | tf_op jit(solution)/shard_map/reduce_scatter | solution.py:45
  1119.1 324.4 %reduce-scatter.23.cloned.1.call-start = ((), (), s32[]{:S(2)}) async-start(), calls=%async_computation.17 | async-start | bytes 21233664 | tf_op jit(solution)/shard_map/reduce_scatter | solution.py:45
  1155.7 408.5 %reduce-scatter.25.cloned.1.call-start = ((), (), s32[]{:S(2)}) async-start(), calls=%async_computation.18 | async-start | bytes 21233664 | tf_op jit(solution)/shard_map/reduce_scatter | solution.py:46
  1201.3 483.5 %reduce-scatter.27.cloned.1.call-start = ((), (), s32[]{:S(2)}) async-start(), calls=%async_computation.19 | async-start | bytes 21233664 | tf_op jit(solution)/shard_map/reduce_scatter | solution.py:46
  1246.5 559.0 %reduce-scatter.29.cloned.1.call-start = ((), (), s32[]{:S(2)}) async-start(), calls=%async_computation.20 | async-start | bytes 21233664 | tf_op jit(solution)/shard_map/reduce_scatter | solution.py:46
  1291.8 634.8 %reduce-scatter.31.cloned.1.call-start = ((), (), s32[]{:S(2)}) async-start(), calls=%async_computation.21 | async-start | bytes 21233664 | tf_op jit(solution)/shard_map/reduce_scatter | solution.py:46
  1337.2 710.0 %reduce-scatter.33.cloned.1.call-start = ((), (), s32[]{:S(2)}) async-start(), calls=%async_computation.22 | async-start | bytes 21233664 | tf_op jit(solution)/shard_map/reduce_scatter | solution.py:46
  1382.8 785.5 %reduce-scatter.35.cloned.1.call-start = ((), (), s32[]{:S(2)}) async-start(), calls=%async_computation.23 | async-start | bytes 21233664 | tf_op jit(solution)/shard_map/reduce_scatter | solution.py:46
  1428.1 884.6 %all-gather.7.cloned.1.call-start = ((), (), s32[]{:S(2)}) async-start(), calls=%async_computation.24 | async-start | bytes 21233664 | tf_op jit(solution)/shard_map/all_gather | solution.py:57
  1438.3 767.6 %copy-start = (bf16[1536,768]{0,1:T(8,128)(2,1)S(1)}, bf16[1536,768]{0,1:T(8,128)(2,1)}, u32[]{:S(2)}) copy-start(bf16[1536,768]{0,1:T(8,128)(2,1)} %reduce-scatter.17.cloned.1.call-done) | copy-start | bytes 7077892
  2201.2 189.7 %all-gather.11.cloned.1.call-start = ((), (), s32[]{:S(2)}) async-start(), calls=%async_computation.26 | async-start | bytes 21233664 | tf_op jit(solution)/shard_map/all_gather | solution.py:57
  2205.9 279.7 %all-gather.9.cloned.1.call-start = ((), (), s32[]{:S(2)}) async-start(), calls=%async_computation.25 | async-start | bytes 21233664 | tf_op jit(solution)/shard_map/all_gather | solution.py:57
  2209.8 9.4 copy-start.1
  2209.8 386.4 %all-gather.13.cloned.1.call-start = ((), (), s32[]{:S(2)}) async-start(), calls=%async_computation.27 | async-start | bytes 21233664 | tf_op jit(solution)/shard_map/all_gather | solution.py:58
  2214.5 460.4 %all-gather.17.cloned.1.call-start = ((), (), s32[]{:S(2)}) async-start(), calls=%async_computation.29 | async-start | bytes 21233664 | tf_op jit(solution)/shard_map/all_gather | solution.py:58
  2219.1 550.5 %all-gather.15.cloned.1.call-start = ((), (), s32[]{:S(2)}) async-start(), calls=%async_computation.28 | async-start | bytes 21233664 | tf_op jit(solution)/shard_map/all_gather | solution.py:58
  2219.1 44.8 %slice-start = ((s8[4718592]{0:T(1024)(128)(4,1)}), s8[524288]{0:T(1024)(128)(4,1)S(1)}, s32[]{:S(2)}) async-start(s8[4718592]{0:T(1024)(128)(4,1)} %bitcast.156), calls=%async_computation.30 | async-start | bytes 1048576
  2223.1 40.9 %slice-start.1 = ((s8[4718592]{0:T(1024)(128)(4,1)}), s8[4194304]{0:T(1024)(128)(4,1)S(1)}, s32[]{:S(2)}) async-start(s8[4718592]{0:T(1024)(128)(4,1)} %bitcast.156), calls=%async_computation.31 | async-start | bytes 8388608
Sparse Core Ops, SparseCore 0:
  420.2 119.8 reduce-scatter.16
  810.0 119.8 reduce-scatter.18
  946.3 119.8 reduce-scatter.12
  1082.6 119.8 reduce-scatter.14
  1205.9 117.0 reduce-scatter.20
  1326.4 117.0 reduce-scatter.22
  1447.1 117.0 reduce-scatter.24
  1567.7 117.0 reduce-scatter.26
  1688.4 117.0 reduce-scatter.28
  1809.4 117.0 reduce-scatter.30
  1930.1 117.0 reduce-scatter.32
  2051.2 117.0 reduce-scatter.34
  2201.4 94.8 all-gather.6
  2297.9 92.9 all-gather.10
  2392.6 92.9 all-gather.8
  2487.2 92.9 all-gather.12
  2581.9 92.9 all-gather.16
  2676.6 92.9 all-gather.14
where the time goes:
time: 2820 us; the launch traced here: 2810 us
  matrix products  1490 us (53%)
  waiting for transfers between devices  1060 us (38%)
  other arithmetic  136 us (5%)
  local copies, waits for them, and re-layouts  85.6 us (3%)
    reduce_scatter x12, waiting for transfers between devices, device_step(): lax.psum_scatter(layer_grad.astype(jnp.bfloat16), 'data', scatter_dimensi...  715 us
    dot_general x6, matrix products, micro_grads(): lax.dot_general(back_grad, w_down[layer_idx], right_dims, preferred_eleme...  356 us
    all_gather x6, waiting for transfers between devices, device_step(): lax.all_gather((part_sum * clip_scale).astype(jnp.bfloat16), 'data', axis...  346 us
    dot_general x6, matrix products, micro_grads(): lax.dot_general(gelu_out, back_grad, token_dims, preferred_element_type=j...  272 us
    dot_general x6, matrix products, micro_grads(): lax.dot_general(pre_grad, w_up[layer_idx], right_dims, preferred_element_...  244 us
    dot_general x6, matrix products, micro_grads(): jnp.dot(hidden, w_up[layer_idx], preferred_element_type=jnp.float32)  228 us
    dot_general x6, matrix products, micro_grads(): lax.dot_general(hidden, pre_grad, token_dims, preferred_element_type=jnp....  219 us
    dot_general x4, matrix products, micro_grads(): jnp.dot(gelu_out, w_down[layer_idx], preferred_element_type=jnp.float32)  170 us
  transfers between devices with their start and end apart: 18, of which 11 were waited for; matrix products, arithmetic and copies ran while one was open for 44% of the time, Pallas kernels for 0%

commit v1 on v0

v1 whole, which is shorter than its diff:
```python
import jax
import jax.numpy as jnp
from jax import lax
from jax.sharding import PartitionSpec as P

FIRST_SPLIT = 2


def gelu_tanh(values):
    return jax.nn.gelu(values, approximate=True)


def matmul(lhs, rhs):
    return jnp.dot(lhs, rhs, preferred_element_type=jnp.float32)


def matmul_tokens(lhs, rhs):
    return lax.dot_general(lhs, rhs, (((0,), (0,)), ((), ())), preferred_element_type=jnp.float32)


def matmul_right(lhs, rhs):
    return lax.dot_general(lhs, rhs, (((1,), (1,)), ((), ())), preferred_element_type=jnp.float32)


def scatter_sum(grad):
    return lax.psum_scatter(grad.astype(jnp.bfloat16), 'data', scatter_dimension=0, tiled=True)


def gather(part):
    return lax.all_gather(part, 'data', axis=0, tiled=True)


def solution(mesh):
    def device_step(acts_in, grad_out, w_up, w_down, clip_norm):
        layer_count, model_width, hidden_width = w_up.shape
        hidden = acts_in.reshape(-1, model_width)
        back_grad = grad_out.reshape(-1, model_width)
        saved_acts = []
        for layer in range(layer_count):
            pre_act = matmul(hidden, w_up[layer]).astype(jnp.bfloat16)
            gelu_out = gelu_tanh(pre_act.astype(jnp.float32)).astype(jnp.bfloat16)
            saved_acts.append((hidden, pre_act, gelu_out))
            if layer < layer_count - 1:
                hidden = (hidden.astype(jnp.float32) + matmul(gelu_out, w_down[layer])).astype(jnp.bfloat16)

        squares = []

        def settle(value, stage_list):
            flat, tree = jax.tree.flatten((value, stage_list))
            return jax.tree.unflatten(tree, lax.optimization_barrier(flat))

        reduced = []
        gathering = []
        settled = {}

        def advance(value, count):
            nonlocal reduced, gathering
            ready, reduced = reduced[:count], reduced[count:]
            value, (parts, full) = settle(value, ([p for _, p in ready], [g for _, g in gathering]))
            settled.update({name: g for (name, _), g in zip(gathering, full)})
            gathering = []
            for (name, _), part in zip(ready, parts):
                squares.append(sum(jnp.sum(jnp.square(p.astype(jnp.float32))) for p in part))
                gathering.append((name, [gather(p) for p in part]))
            return value

        last = layer_count - 1
        for layer in range(last, -1, -1):
            hidden, pre_act, gelu_out = saved_acts[layer]
            pieces = FIRST_SPLIT if layer == last else 1
            width = hidden_width // pieces
            reduced.append((
                ('down', layer),
                [scatter_sum(matmul_tokens(gelu_out[:, i * width:(i + 1) * width], back_grad)) for i in range(pieces)],
            ))
            act_grad = matmul_right(back_grad, w_down[layer])
            gelu_back = jax.vjp(gelu_tanh, pre_act.astype(jnp.float32))[1]
            pre_grad = gelu_back(act_grad)[0].astype(jnp.bfloat16)
            pre_grad = advance(pre_grad, 1)
            if layer == 0:
                zero, pre_grad = settle(jnp.zeros((), jnp.bfloat16), pre_grad)
                buffers = (jnp.broadcast_to(zero, w_up.shape), jnp.broadcast_to(zero, w_down.shape))
                pre_grad, buffers = settle(pre_grad, buffers)
            reduced.append((('up', layer), [scatter_sum(matmul_tokens(hidden, pre_grad))]))
            back_grad = (back_grad.astype(jnp.float32) + matmul_right(pre_grad, w_up[layer])).astype(jnp.bfloat16)
            if 0 < layer < last:
                back_grad = advance(back_grad, 1)

        for name, part in reduced:
            squares.append(sum(jnp.sum(jnp.square(p.astype(jnp.float32))) for p in part))
            gathering.append((name, [gather(p) for p in part]))
        settled.update(gathering)
        sq_total = lax.psum(sum(squares), 'data')
        clip_scale = jnp.minimum(1.0, clip_norm[0] * lax.rsqrt(sq_total))

        def scaled(values):
            return (values.astype(jnp.float32) * clip_scale).astype(jnp.bfloat16)

        grads = {'up': buffers[0], 'down': buffers[1]}
        for (kind, layer), pieces in settled.items():
            row = 0
            for piece in pieces:
                grads[kind] = lax.dynamic_update_slice(grads[kind], scaled(piece)[None], (layer, row, 0))
                row += piece.shape[0]
        return grads['up'], grads['down'], back_grad.reshape(acts_in.shape)

    return jax.shard_map(
        device_step,
        mesh=mesh,
        in_specs=(P('data'), P('data'), P(), P(), P()),
        out_specs=(P(), P(), P('data')),
        check_vma=False,
    )
```

time: 2820 us -> 1790 us (0.63)
  waiting for transfers between devices: 1060 us -> 221 us
  matrix products: 1490 us -> 1360 us
  local copies, waits for them, and re-layouts: 85.6 us -> 38.8 us
    reduce_scatter x12 -> x7, waiting for transfers between devices: 715 us -> 151 us  [scatter_sum(): lax.psum_scatter(grad.astype(jnp.bfloat16), 'data', scatter_dimension=0,...]
    all_gather x6 -> x7, waiting for transfers between devices: 346 us -> 68.4 us  [gather(): return lax.all_gather(part, 'data', axis=0, tiled=True)]
    dot_general x34 -> x18, matrix products: 1490 us -> 1360 us  [the longest x6 541 us: matmul_right(): lax.dot_general(lhs, rhs, (((1,), (1,)), ((), ())), preferred_element_typ...]
    dynamic_update_slice x0 -> x7, other arithmetic: none -> 100 us  [device_step(): lax.dynamic_update_slice(grads[kind], scaled(piece)[None], (layer, row, 0))]
    another operation x3 -> x0, other arithmetic: 84.5 us -> none  [the longest x2 76.1 us: device_step(): jnp.stack([lax.all_gather((part_sum * clip_scale).astype(jnp.bfloat16), '...]
    unnamed x11 -> x14, local copies, waits for them, and re-layouts: 72.6 us -> 0.03 us
    broadcast_in_dim x0 -> x2, local copies, waits for them, and re-layouts: none -> 38.8 us  [the longest x1 20.8 us: device_step(): jnp.broadcast_to(zero, w_up.shape)]
  transfers between devices with their start and end apart: 18 -> 14, of which waited for: 11 -> 3; matrix products, arithmetic and copies ran while one was open for 44% -> 61% of each run, Pallas kernels for 0% -> 0%
where the time goes in v1:
time: 1790 us; the launch traced here: 1780 us
  matrix products  1360 us (76%)
  waiting for transfers between devices  221 us (12%)
  other arithmetic  119 us (7%)
  local copies, waits for them, and re-layouts  38.8 us (2%)
  blocking collectives  22.9 us (1%)
  between operations  19.9 us (1%)
    dot_general x6, matrix products, matmul_right(): lax.dot_general(lhs, rhs, (((1,), (1,)), ((), ())), preferred_element_typ...  541 us
    dot_general x7, matrix products, matmul_tokens(): lax.dot_general(lhs, rhs, (((0,), (0,)), ((), ())), preferred_element_typ...  444 us
    dot_general x5, matrix products, matmul(): return jnp.dot(lhs, rhs, preferred_element_type=jnp.float32)  374 us
    reduce_scatter x7, waiting for transfers between devices, scatter_sum(): lax.psum_scatter(grad.astype(jnp.bfloat16), 'data', scatter_dimension=0,...  151 us
    dynamic_update_slice x7, other arithmetic, device_step(): lax.dynamic_update_slice(grads[kind], scaled(piece)[None], (layer, row, 0))  100 us
    all_gather x7, waiting for transfers between devices, gather(): return lax.all_gather(part, 'data', axis=0, tiled=True)  68.4 us
  transfers between devices with their start and end apart: 14, of which 3 were waited for; matrix products, arithmetic and copies ran while one was open for 61% of the time, Pallas kernels for 0%

profile of v1, /device:TPU:0, one launch (start us, length us, event | category | flops | bytes accessed | tf_op | source)
XLA Modules:
  0.0 1781.0 jit_solution(16543788614311671786)
XLA Ops:
  7.2 66.9 %convolution_convert_fusion.2 = bf16[3072,6144]{1,0:T(8,128)(2,1)} fusion(bf16[3072,1536]{1,0:T(8,128)(2,1)} %bitcast.134, bf16[3,1536,6144]{2,1,0:T(8,128)(2,1)} %param.7), kind=kOutput, calls=%fused_computation.52 | convolution fusion | flops 58000932864 | bytes 66060288 | tf_op jit(solution)/shard_map/dot_general | solution.py:14
  74.1 76.8 %add_convert_fusion.4 = bf16[3072,1536]{1,0:T(8,128)(2,1)} fusion(bf16[3072,1536]{1,0:T(8,128)(2,1)} %bitcast.135, bf16[3,6144,1536]{2,1,0:T(8,128)(2,1)} %param.8, bf16[3072,6144]{1,0:T(8,128)(2,1)} %convolution_convert_fusion.2), kind=kOutput, calls=%fused_computation.95 | convolution fusion | flops 58184957952 | bytes 75497472 | tf_op jit(solution)/shard_map/dot_general | solution.py:14
  150.9 67.2 %convolution_convert_fusion.1 = bf16[3072,6144]{1,0:T(8,128)(2,1)} fusion(bf16[3072,1536]{1,0:T(8,128)(2,1)} %add_convert_fusion.4, bf16[3,1536,6144]{2,1,0:T(8,128)(2,1)} %param.7), kind=kOutput, calls=%fused_computation.51 | convolution fusion | flops 58000932864 | bytes 66060288 | tf_op jit(solution)/shard_map/dot_general | solution.py:14
  218.1 77.1 %add_convert_fusion.3 = bf16[3072,1536]{1,0:T(8,128)(2,1)} fusion(bf16[3072,1536]{1,0:T(8,128)(2,1)} %add_convert_fusion.4, bf16[3,6144,1536]{2,1,0:T(8,128)(2,1)} %param.8, bf16[3072,6144]{1,0:T(8,128)(2,1)} %convolution_convert_fusion.1), kind=kOutput, calls=%fused_computation.94 | convolution fusion | flops 58184957952 | bytes 75497472 | tf_op jit(solution)/shard_map/dot_general | solution.py:14
  295.2 86.4 %fusion.29 = (bf16[3072,6144]{1,0:T(8,128)(2,1)}, bf16[3072,6144]{1,0:T(8,128)(2,1)}) fusion(bf16[3072,1536]{1,0:T(8,128)(2,1)} %add_convert_fusion.3, bf16[3,1536,6144]{2,1,0:T(8,128)(2,1)} %param.7), kind=kOutput, calls=%fused_computation.44 | convolution fusion | flops 58189676544 | bytes 103809024 | tf_op jit(solution)/shard_map/dot_general | solution.py:14
  381.7 36.8 %fusion.72 = bf16[3072,1536]{1,0:T(8,128)(2,1)} fusion(bf16[3072,1536]{1,0:T(8,128)(2,1)} %bitcast.130, bf16[3072,6144]{1,0:T(8,128)(2,1)} %get-tuple-element.39), kind=kOutput, calls=%fused_computation.107 | convolution fusion | flops 28995747840 | bytes 37748736 | tf_op jit(solution)/shard_map/dot_general | solution.py:18
  418.5 36.8 %fusion.75 = bf16[3072,1536]{1,0:T(8,128)(2,1)} fusion(bf16[3072,1536]{1,0:T(8,128)(2,1)} %bitcast.131, bf16[3072,6144]{1,0:T(8,128)(2,1)} %get-tuple-element.39), kind=kOutput, calls=%fused_computation.108 | convolution fusion | flops 28995747840 | bytes 37748736 | tf_op jit(solution)/shard_map/dot_general | solution.py:18
  455.4 112.1 %fusion.5 = bf16[3072,6144]{1,0:T(8,128)(2,1)} fusion(bf16[3072,6144]{1,0:T(8,128)(2,1)} %get-tuple-element.40, bf16[3072,1536]{1,0:T(8,128)(2,1)} %bitcast.132, bf16[3,6144,1536]{2,1,0:T(8,128)(2,1)} %param.8), kind=kOutput, calls=%fused_computation.20 | convolution fusion | flops 58378420224 | bytes 103809024 | tf_op jit(solution)/shard_map/dot_general | solution.py:22
  568.2 67.6 %convolution_convert_fusion.7 = bf16[1536,6144]{1,0:T(8,128)(2,1)} fusion(bf16[3072,1536]{1,0:T(8,128)(2,1)} %add_convert_fusion.3, bf16[3072,6144]{1,0:T(8,128)(2,1)} %fusion.5), kind=kOutput, calls=%fused_computation.57 | convolution fusion | flops 57991495680 | bytes 66060288 | tf_op jit(solution)/shard_map/dot_general | solution.py:18
  635.8 68.3 %add_convert_fusion.2 = bf16[3072,1536]{1,0:T(8,128)(2,1)} fusion(bf16[3072,1536]{1,0:T(8,128)(2,1)} %bitcast.133, bf16[3072,6144]{1,0:T(8,128)(2,1)} %fusion.5, bf16[3,1536,6144]{2,1,0:T(8,128)(2,1)} %param.7), kind=kOutput, calls=%fused_computation.93 | convolution fusion | flops 57996214272 | bytes 75497472 | tf_op jit(solution)/shard_map/dot_general | solution.py:22
  704.2 83.8 %convolution_convert_fusion.6 = bf16[6144,1536]{1,0:T(8,128)(2,1)} fusion(bf16[3072,1536]{1,0:T(8,128)(2,1)} %add_convert_fusion.2, bf16[3072,6144]{1,0:T(8,128)(2,1)} %convolution_convert_fusion.1), kind=kOutput, calls=%fused_computation.56 | convolution fusion | flops 58180239360 | bytes 66060288 | tf_op jit(solution)/shard_map/dot_general | solution.py:18
  788.0 112.0 %fusion.8 = bf16[3072,6144]{1,0:T(8,128)(2,1)} fusion(bf16[3072,6144]{1,0:T(8,128)(2,1)} %convolution_convert_fusion.1, bf16[3072,1536]{1,0:T(8,128)(2,1)} %add_convert_fusion.2, bf16[3,6144,1536]{2,1,0:T(8,128)(2,1)} %param.8), kind=kOutput, calls=%fused_computation.23 | convolution fusion | flops 58378420224 | bytes 103809024 | tf_op jit(solution)/shard_map/dot_general | solution.py:22
  900.1 67.6 %convolution_convert_fusion.5 = bf16[1536,6144]{1,0:T(8,128)(2,1)} fusion(bf16[3072,1536]{1,0:T(8,128)(2,1)} %add_convert_fusion.4, bf16[3072,6144]{1,0:T(8,128)(2,1)} %fusion.8), kind=kOutput, calls=%fused_computation.55 | convolution fusion | flops 57991495680 | bytes 66060288 | tf_op jit(solution)/shard_map/dot_general | solution.py:18
  967.8 68.3 %add_convert_fusion.1 = bf16[3072,1536]{1,0:T(8,128)(2,1)} fusion(bf16[3072,1536]{1,0:T(8,128)(2,1)} %add_convert_fusion.2, bf16[3072,6144]{1,0:T(8,128)(2,1)} %fusion.8, bf16[3,1536,6144]{2,1,0:T(8,128)(2,1)} %param.7), kind=kOutput, calls=%fused_computation.92 | convolution fusion | flops 57996214272 | bytes 75497472 | tf_op jit(solution)/shard_map/dot_general | solution.py:22
  1036.2 83.9 %convolution_convert_fusion.4 = bf16[6144,1536]{1,0:T(8,128)(2,1)} fusion(bf16[3072,1536]{1,0:T(8,128)(2,1)} %add_convert_fusion.1, bf16[3072,6144]{1,0:T(8,128)(2,1)} %convolution_convert_fusion.2), kind=kOutput, calls=%fused_computation.54 | convolution fusion | flops 58180239360 | bytes 66060288 | tf_op jit(solution)/shard_map/dot_general | solution.py:18
  1120.2 111.8 %fusion.11 = bf16[3072,6144]{1,0:T(8,128)(2,1)} fusion(bf16[3072,6144]{1,0:T(8,128)(2,1)} %convolution_convert_fusion.2, bf16[3072,1536]{1,0:T(8,128)(2,1)} %add_convert_fusion.1, bf16[3,6144,1536]{2,1,0:T(8,128)(2,1)} %param.8), kind=kOutput, calls=%fused_computation.26 | convolution fusion | flops 58378420224 | bytes 103809024 | tf_op jit(solution)/shard_map/dot_general | solution.py:22
  1232.0 67.6 %fusion.30 = bf16[1536,6144]{1,0:T(8,128)(2,1)} fusion(bf16[3072,6144]{1,0:T(8,128)(2,1)} %fusion.11, bf16[3072,1536]{1,0:T(8,128)(2,1)} %bitcast.136), kind=kOutput, calls=%fused_computation.58 | convolution fusion | flops 57991495680 | bytes 66060288 | tf_op jit(solution)/shard_map/dot_general | solution.py:18
  1299.7 50.7 %reduce-scatter.18.cloned.1.call-done = bf16[768,1536]{1,0:T(8,128)(2,1)} async-done(((bf16[6144,1536]{1,0:T(8,128)(2,1)}), bf16[768,1536]{1,0:T(8,128)(2,1)}) %reduce-scatter.18.cloned.1.call-update) | async-done | bytes 2359312 | tf_op jit(solution)/shard_map/reduce_scatter | solution.py:26
  1370.7 100.3 %reduce-scatter.20.cloned.1.call-done = bf16[192,6144]{1,0:T(8,128)(2,1)} async-done(((bf16[1536,6144]{1,0:T(8,128)(2,1)}), bf16[192,6144]{1,0:T(8,128)(2,1)}) %reduce-scatter.20.cloned.1.call-update) | async-done | bytes 2359312 | tf_op jit(solution)/shard_map/reduce_scatter | solution.py:26
  1475.2 68.1 %add_convert_fusion = bf16[3072,1536]{1,0:T(8,128)(2,1)} fusion(bf16[3072,1536]{1,0:T(8,128)(2,1)} %add_convert_fusion.1, bf16[3072,6144]{1,0:T(8,128)(2,1)} %fusion.11, bf16[3,1536,6144]{2,1,0:T(8,128)(2,1)} %param.7), kind=kOutput, calls=%fused_computation.89 | convolution fusion | flops 57996214272 | bytes 75497472 | tf_op jit(solution)/shard_map/dot_general | solution.py:22
  1543.3 22.9 %psum.7 = f32[]{:T(128)} all-reduce(f32[]{:T(128)S(6)} %add.91), channel_id=1, replica_groups=mesh['data'=8] {'data'}, use_global_device_ids=true, to_apply=%region_14.0 | all-reduce | flops 1 | bytes 8 | tf_op jit(solution)/shard_map/psum | solution.py:93
  1603.4 20.8 %broadcast_in_dim.27 = bf16[3,1536,6144]{2,1,0:T(8,128)(2,1)} broadcast(bf16[]{:T(256)} %constant.3.clone.1), dimensions={} | broadcast | bytes 56623104 | tf_op jit(solution)/shard_map/broadcast_in_dim | solution.py:82
  1624.2 19.3 %fusion.32 = bf16[3,1536,6144]{2,1,0:T(8,128)(2,1)} fusion(bf16[3,1536,6144]{2,1,0:T(8,128)(2,1)} %broadcast_in_dim.27, bf16[1536,6144]{1,0:T(8,128)(2,1)} %all-gather.12.cloned.1.call-done, f32[]{:T(128)S(6)} %min.3), kind=kLoop, calls=%fused_computation.60 | loop fusion | flops 28311552 | bytes 37748740 | tf_op jit(solution)/shard_map/dynamic_update_slice | solution.py:103
  1687.9 68.3 %all-gather.18.cloned.1.call-done = bf16[1536,6144]{1,0:T(8,128)(2,1)} async-done(((bf16[192,6144]{1,0:T(8,128)(2,1)}), bf16[1536,6144]{1,0:T(8,128)(2,1)}) %all-gather.18.cloned.1.call-update) | async-done | bytes 18874384 | tf_op jit(solution)/shard_map/all_gather | solution.py:30
  (67 shorter events, 119.7 us)
Async XLA Ops:
  7.2 560.3 %reduce-scatter.8.cloned.1.call-start = ((), (), s32[]{:S(2)}) async-start(), calls=%async_computation.7 | async-start | bytes 10616832 | tf_op jit(solution)/shard_map/reduce_scatter | solution.py:26
  418.5 149.0 %reduce-scatter.10.cloned.1.call-start = ((), (), s32[]{:S(2)}) async-start(), calls=%async_computation.8 | async-start | bytes 10616832 | tf_op jit(solution)/shard_map/reduce_scatter | solution.py:26
  455.4 444.7 %all-gather.8.cloned.1.call-start = ((), (), s32[]{:S(2)}) async-start(), calls=%async_computation.10 | async-start | bytes 10616832 | tf_op jit(solution)/shard_map/all_gather | solution.py:30
  567.6 332.5 %all-gather.10.cloned.1.call-start = ((), (), s32[]{:S(2)}) async-start(), calls=%async_computation.11 | async-start | bytes 10616832 | tf_op jit(solution)/shard_map/all_gather | solution.py:30
  568.1 331.9 %reduce-scatter.12.cloned.1.call-start = ((), (), s32[]{:S(2)}) async-start(), calls=%async_computation.9 | async-start | bytes 21233664 | tf_op jit(solution)/shard_map/reduce_scatter | solution.py:26
  635.8 400.3 %reduce-scatter.14.cloned.1.call-start = ((), (), s32[]{:S(2)}) async-start(), calls=%async_computation.12 | async-start | bytes 21233664 | tf_op jit(solution)/shard_map/reduce_scatter | solution.py:26
  787.9 248.2 %all-gather.12.cloned.1.call-start = ((), (), s32[]{:S(2)}) async-start(), calls=%async_computation.13 | async-start | bytes 21233664 | tf_op jit(solution)/shard_map/all_gather | solution.py:30
  900.1 331.9 %reduce-scatter.16.cloned.1.call-start = ((), (), s32[]{:S(2)}) async-start(), calls=%async_computation.14 | async-start | bytes 21233664 | tf_op jit(solution)/shard_map/reduce_scatter | solution.py:26
  967.7 264.3 %all-gather.14.cloned.1.call-start = ((), (), s32[]{:S(2)}) async-start(), calls=%async_computation.15 | async-start | bytes 21233664 | tf_op jit(solution)/shard_map/all_gather | solution.py:30
  1036.1 314.2 %reduce-scatter.18.cloned.1.call-start = ((), (), s32[]{:S(2)}) async-start(), calls=%async_computation.16 | async-start | bytes 21233664 | tf_op jit(solution)/shard_map/reduce_scatter | solution.py:26
  1120.1 350.9 %reduce-scatter.20.cloned.1.call-start = ((), (), s32[]{:S(2)}) async-start(), calls=%async_computation.17 | async-start | bytes 21233664 | tf_op jit(solution)/shard_map/reduce_scatter | solution.py:26
  1232.0 120.2 %copy-start.1 = (bf16[384,1536]{1,0:T(8,128)(2,1)S(1)}, bf16[384,1536]{1,0:T(8,128)(2,1)}, u32[]{:S(2)}) copy-start(bf16[384,1536]{1,0:T(8,128)(2,1)} %reduce-scatter.8.cloned.1.call-done) | copy-start | bytes 3538948
  1232.0 135.8 %copy-start = (bf16[192,6144]{1,0:T(8,128)(2,1)S(1)}, bf16[192,6144]{1,0:T(8,128)(2,1)}, u32[]{:S(2)}) copy-start(bf16[192,6144]{1,0:T(8,128)(2,1)} %reduce-scatter.16.cloned.1.call-done) | copy-start | bytes 7077892
  1299.6 352.6 %all-gather.20.cloned.1.call-start = ((), (), s32[]{:S(2)}) async-start(), calls=%async_computation.20 | async-start | bytes 21233664 | tf_op jit(solution)/shard_map/all_gather | solution.py:30
  1350.4 319.5 %all-gather.16.cloned.1.call-start = ((), (), s32[]{:S(2)}) async-start(), calls=%async_computation.18 | async-start | bytes 21233664 | tf_op jit(solution)/shard_map/all_gather | solution.py:30
  1351.1 405.1 %all-gather.18.cloned.1.call-start = ((), (), s32[]{:S(2)}) async-start(), calls=%async_computation.19 | async-start | bytes 21233664 | tf_op jit(solution)/shard_map/all_gather | solution.py:30
  1603.4 40.2 %slice-start = ((s8[18874368]{0:T(1024)(128)(4,1)}), s8[4194304]{0:T(1024)(128)(4,1)S(1)}, s32[]{:S(2)}) async-start(s8[18874368]{0:T(1024)(128)(4,1)} %bitcast.128), calls=%async_computation.21 | async-start | bytes 8388608
  1603.4 40.2 %slice-start.1 = ((s8[18874368]{0:T(1024)(128)(4,1)}), s8[4194304]{0:T(1024)(128)(4,1)S(1)}, s32[]{:S(2)}) async-start(s8[18874368]{0:T(1024)(128)(4,1)} %bitcast.128), calls=%async_computation.22 | async-start | bytes 8388608
  1603.4 40.2 %slice-start.2 = ((s8[18874368]{0:T(1024)(128)(4,1)}), s8[2097152]{0:T(1024)(128)(4,1)S(1)}, s32[]{:S(2)}) async-start(s8[18874368]{0:T(1024)(128)(4,1)} %bitcast.128), calls=%async_computation.23 | async-start | bytes 4194304
  1624.2 19.4 %slice-start.3 = ((s8[18874368]{0:T(1024)(128)(4,1)}), s8[4194304]{0:T(1024)(128)(4,1)S(1)}, s32[]{:S(2)}) async-start(s8[18874368]{0:T(1024)(128)(4,1)} %bitcast.128), calls=%async_computation.24 | async-start | bytes 8388608
  1624.2 19.4 %slice-start.4 = ((s8[18874368]{0:T(1024)(128)(4,1)}), s8[4194304]{0:T(1024)(128)(4,1)S(1)}, s32[]{:S(2)}) async-start(s8[18874368]{0:T(1024)(128)(4,1)} %bitcast.128), calls=%async_computation.25 | async-start | bytes 8388608
Sparse Core Ops, SparseCore 0:
  418.6 70.2 reduce-scatter.7
  492.3 67.4 reduce-scatter.9
  567.7 55.7 all-gather.7
  625.1 52.9 all-gather.9
  681.5 117.0 reduce-scatter.11
  802.0 117.0 reduce-scatter.13
  920.9 92.9 all-gather.11
  1017.4 117.0 reduce-scatter.15
  1136.3 92.9 all-gather.13
  1233.3 117.0 reduce-scatter.17
  1353.9 117.0 reduce-scatter.19
  1472.7 94.0 all-gather.19
  1568.5 92.9 all-gather.15
  1663.2 92.9 all-gather.17
